TPU v7x, 32 devices: a whole 2x2x4 slice. The times are simulated.
32 devices in a mesh: head: 4 (over y, core), blk: 8 (over z, x).
Axes of the slice: x: 2, y: 2, z: 4, core: 2. Of those that a mesh axis runs over, the one named last changes fastest.
Arguments:
- block_input: bfloat16 [4096, 1024], P(('head', 'blk')), may hold values from -6 to 6
- span_order: int32 [32], replicated, may hold values from 0 to 31, each once
- norm1_gain: bfloat16 [1024], P(('head', 'blk')), may hold values from 0.099609375 to 1.8984375
- w_query: bfloat16 [1024, 1024], P(('head', 'blk')), may hold values from -0.1875 to 0.1875
- key_weight: bfloat16 [1024, 512], P(('head', 'blk')), may hold values from -0.1875 to 0.1875
- value_weight: bfloat16 [1024, 512], P(('head', 'blk')), may hold values from -0.1875 to 0.1875
- qk_gain: float32 [2, 64], replicated, may hold values from 0.5 to 3, as said below
- w_out: bfloat16 [1024, 1024], P(('head', 'blk')), may hold values from -6 to 6
- norm2_gain: bfloat16 [1024], P(('head', 'blk')), may hold values from 0.099609375 to 1.8984375
- w_gate: bfloat16 [1024, 4608], P(('head', 'blk')), may hold values from -0.1875 to 0.1875
- w_up: bfloat16 [1024, 4608], P(('head', 'blk')), may hold values from -0.1875 to 0.1875
- w_down: bfloat16 [4608, 1024], P(('head', 'blk')), may hold values from -0.09375 to 0.09375
- out_grad: bfloat16 [4096, 1024], P(('head', 'blk')), may hold values from -6 to 6
Outputs:
- block_output: bfloat16 [4096, 1024], P(('head', 'blk'))
- input_grad: bfloat16 [4096, 1024], P(('head', 'blk'))
- norm1_grad: float32 [1024], P(('head', 'blk'))
- query_grad: float32 [1024, 1024], P(('head', 'blk'))
- key_grad: float32 [1024, 512], P(('head', 'blk'))
- value_grad: float32 [1024, 512], P(('head', 'blk'))
- qk_gain_grad: float32 [2, 64], replicated
- out_proj_grad: float32 [1024, 1024], P(('head', 'blk'))
- norm2_grad: float32 [1024], P(('head', 'blk'))
- gate_grad: float32 [1024, 4608], P(('head', 'blk'))
- up_grad: float32 [1024, 4608], P(('head', 'blk'))
- down_grad: float32 [4608, 1024], P(('head', 'blk'))
Inputs may be any that keep to these rules, and one draw needn't show every extreme that they name: Storage span c of 128 rows holds the sequence positions from span_order[c] * 128 on; every span place occurs once. `qk_gain`: positive gains.
All inputs are finite; a program needn't handle non-finite values.
Results may differ from a plain program's by a relative error of at most 0.02.
The roundings to bfloat16 on the way count: a program that leaves them out, or rounds other values in their place, can miss the bound.
Values may be sent and summed in bfloat16 or wider, within the bound.
A program may use at most 512 MiB of HBM per device.

v0:
```python
import math
import jax
import jax.numpy as jnp
from jax import lax
from jax.sharding import PartitionSpec as P

EPS = 1e-05
THETA = 1000000.0
NEG = -1e30


def rms_norm(values, gain_vec):
    inverse = lax.rsqrt(jnp.mean(values * values, axis=-1, keepdims=True) + EPS)
    return values * inverse * gain_vec


def rotate(field_in, where_at):
    half_size = field_in.shape[-1] // 2
    frequency = jnp.exp(
        jnp.arange(half_size, dtype=jnp.float32)
        * jnp.float32(-2.0 * math.log(THETA) / field_in.shape[-1])
    )
    angles = where_at.astype(jnp.float32)[:, None] * frequency[None, :]
    cosine = jnp.cos(angles)[:, None, :]
    sine_part = jnp.sin(angles)[:, None, :]
    first_half = field_in[..., :half_size]
    second_half = field_in[..., half_size:]
    return jnp.concatenate(
        [
            first_half * cosine - second_half * sine_part,
            second_half * cosine + first_half * sine_part,
        ],
        axis=-1,
    )


def head_map(raw_rows, gain_vec, where_at):
    row_count = raw_rows.shape[0]
    shaped = raw_rows.reshape(row_count, -1, gain_vec.shape[0])
    return rotate(rms_norm(shaped, gain_vec), where_at).reshape(row_count, -1)


def lookup(span_ids, order_table):
    matches = span_ids[:, None] == jnp.arange(order_table.shape[0], dtype=jnp.int32)[None, :]
    return jnp.sum(jnp.where(matches, order_table[None, :], 0), axis=1)


def positions(row_ids, tok_rows, blocks, group_rows, order_table):
    span_ids = row_ids % group_rows // tok_rows * blocks + row_ids // group_rows
    return lookup(span_ids, order_table) * tok_rows + row_ids % tok_rows


def local(
    block_input,
    span_order,
    norm1_gain,
    w_query,
    key_weight,
    value_weight,
    qk_gain,
    w_out,
    norm2_gain,
    w_gate,
    w_up,
    w_down,
    out_grad,
):
    blocks = lax.axis_size("blk")
    groups = lax.axis_size("head")
    tok_rows = block_input.shape[0]
    group_rows = groups * tok_rows
    head_size = qk_gain.shape[1]
    kv_total = key_weight.shape[1] // head_size
    kv_local = kv_total // groups
    share_count = w_query.shape[1] // key_weight.shape[1]
    score_scale = float(head_size) ** (-0.5)
    blk_index = lax.axis_index("blk")
    head_index = lax.axis_index("head")
    own_rows = (
        blk_index * group_rows + head_index * tok_rows + jnp.arange(tok_rows, dtype=jnp.int32)
    )
    tok_where = positions(own_rows, tok_rows, blocks, group_rows, span_order)
    query_where = positions(
        blk_index * group_rows + jnp.arange(group_rows, dtype=jnp.int32),
        tok_rows,
        blocks,
        group_rows,
        span_order,
    )
    gathered = (
        lax.all_gather(norm1_gain, ("head", "blk"), axis=0, tiled=True),
        lax.all_gather(w_query, ("head", "blk"), axis=0, tiled=True),
        lax.all_gather(key_weight, ("head", "blk"), axis=0, tiled=True),
        lax.all_gather(value_weight, ("head", "blk"), axis=0, tiled=True),
        lax.all_gather(w_out, ("head", "blk"), axis=0, tiled=True),
        lax.all_gather(norm2_gain, ("head", "blk"), axis=0, tiled=True),
        lax.all_gather(w_gate, ("head", "blk"), axis=0, tiled=True),
        lax.all_gather(w_up, ("head", "blk"), axis=0, tiled=True),
        lax.all_gather(w_down, ("head", "blk"), axis=0, tiled=True),
    )
    (
        gain_one,
        query_full,
        key_full,
        value_full,
        out_full,
        gain_two,
        gate_full,
        up_full,
        down_full,
    ) = gathered
    gain_one = gain_one.astype(jnp.float32)
    gain_two = gain_two.astype(jnp.float32)
    in_flat = block_input.astype(jnp.float32)
    normed = rms_norm(in_flat, gain_one).astype(jnp.bfloat16)
    q_raw = jnp.dot(normed, query_full, preferred_element_type=jnp.float32)
    k_raw = jnp.dot(normed, key_full, preferred_element_type=jnp.float32)
    v_raw = jnp.dot(normed, value_full, preferred_element_type=jnp.float32)

    def query_map(raw_rows, gain_vec):
        return head_map(raw_rows, gain_vec, tok_where)

    queries = query_map(q_raw, qk_gain[0]).astype(jnp.bfloat16)
    keys = query_map(k_raw, qk_gain[1]).astype(jnp.bfloat16)
    values = v_raw.astype(jnp.bfloat16)
    q_heads, k_heads, v_heads = (
        lax.all_to_all(queries, "head", split_axis=1, concat_axis=0, tiled=True),
        lax.all_to_all(keys, "head", split_axis=1, concat_axis=0, tiled=True),
        lax.all_to_all(values, "head", split_axis=1, concat_axis=0, tiled=True),
    )
    q_four = q_heads.reshape(group_rows, kv_local, share_count, head_size)

    def key_where(row_count):
        return positions(
            jnp.arange(row_count, dtype=jnp.int32), tok_rows, blocks, group_rows, span_order
        )

    start_state = (
        jnp.full((kv_local, share_count, group_rows), NEG, jnp.float32),
        jnp.zeros((kv_local, share_count, group_rows), jnp.float32),
        jnp.zeros((group_rows, kv_local, share_count, head_size), jnp.float32),
    )
    key_piece = lax.all_gather(k_heads, "blk", axis=0, tiled=True)
    value_piece = lax.all_gather(v_heads, "blk", axis=0, tiled=True)
    row_count = key_piece.shape[0]
    key_three = key_piece.reshape(row_count, kv_local, head_size)
    value_three = value_piece.reshape(row_count, kv_local, head_size)
    causal = key_where(row_count)[None, :] <= query_where[:, None]

    def update(held_state):
        row_max, row_sum, accumulated = held_state
        scores = (
            jnp.einsum("qkgd,nkd->kgqn", q_four, key_three, preferred_element_type=jnp.float32)
            * score_scale
        )
        scores = jnp.where(causal, scores, NEG)
        new_max = jnp.maximum(row_max, jnp.max(scores, axis=-1))
        weights = jnp.where(causal, jnp.exp(scores - new_max[..., None]), 0.0)
        row_sum = jnp.sum(weights, axis=-1)
        value_part = jnp.einsum(
            "kgqn,nkd->qkgd",
            weights.astype(jnp.bfloat16),
            value_three,
            preferred_element_type=jnp.float32,
        )
        accumulated = value_part
        return (new_max, row_sum, accumulated)

    row_max, row_sum, accumulated = update(start_state)
    attended_heads = (accumulated / row_sum.transpose(2, 0, 1)[..., None]).astype(jnp.bfloat16)
    log_total = row_max + jnp.log(row_sum)
    attended = lax.all_to_all(
        attended_heads.reshape(group_rows, -1), "head", split_axis=0, concat_axis=1, tiled=True
    )
    middle = in_flat + jnp.dot(attended, out_full, preferred_element_type=jnp.float32)
    normed2 = rms_norm(middle, gain_two).astype(jnp.bfloat16)
    gate_rows = jnp.dot(normed2, gate_full, preferred_element_type=jnp.float32)
    up_rows = jnp.dot(normed2, up_full, preferred_element_type=jnp.float32)
    hidden = (jax.nn.silu(gate_rows) * up_rows).astype(jnp.bfloat16)
    block_output = (middle + jnp.dot(hidden, down_full, preferred_element_type=jnp.float32)).astype(
        jnp.bfloat16
    )
    gathered = (
        lax.all_gather(norm1_gain, ("head", "blk"), axis=0, tiled=True),
        lax.all_gather(w_query, ("head", "blk"), axis=0, tiled=True),
        lax.all_gather(key_weight, ("head", "blk"), axis=0, tiled=True),
        lax.all_gather(value_weight, ("head", "blk"), axis=0, tiled=True),
        lax.all_gather(w_out, ("head", "blk"), axis=0, tiled=True),
        lax.all_gather(norm2_gain, ("head", "blk"), axis=0, tiled=True),
        lax.all_gather(w_gate, ("head", "blk"), axis=0, tiled=True),
        lax.all_gather(w_up, ("head", "blk"), axis=0, tiled=True),
        lax.all_gather(w_down, ("head", "blk"), axis=0, tiled=True),
    )
    (
        gain_one,
        query_full,
        key_full,
        value_full,
        out_full,
        gain_two,
        gate_full,
        up_full,
        down_full,
    ) = gathered
    gain_one = gain_one.astype(jnp.float32)
    gain_two = gain_two.astype(jnp.float32)
    dhidden = jnp.dot(out_grad, down_full.T, preferred_element_type=jnp.float32)
    down_grad = jnp.dot(hidden.T, out_grad, preferred_element_type=jnp.float32)
    _, gate_back = jax.vjp(lambda gate_in, up_in: jax.nn.silu(gate_in) * up_in, gate_rows, up_rows)
    dgate, dup = gate_back(dhidden)
    dgate = dgate.astype(jnp.bfloat16)
    dup = dup.astype(jnp.bfloat16)
    dnormed2 = jnp.dot(dgate, gate_full.T, preferred_element_type=jnp.float32) + jnp.dot(
        dup, up_full.T, preferred_element_type=jnp.float32
    )
    gate_grad = jnp.dot(normed2.T, dgate, preferred_element_type=jnp.float32)
    up_grad = jnp.dot(normed2.T, dup, preferred_element_type=jnp.float32)
    _, norm2_back = jax.vjp(rms_norm, middle, gain_two)
    dmiddle_norm, norm2_grad = norm2_back(dnormed2)
    dmiddle = out_grad.astype(jnp.float32) + dmiddle_norm
    dmiddle_b = dmiddle.astype(jnp.bfloat16)
    out_proj_grad = jnp.dot(attended.T, dmiddle_b, preferred_element_type=jnp.float32)
    dattended = jnp.dot(dmiddle_b, out_full.T, preferred_element_type=jnp.float32).astype(
        jnp.bfloat16
    )
    grad_heads = lax.all_to_all(dattended, "head", split_axis=1, concat_axis=0, tiled=True)
    grad_four = grad_heads.reshape(group_rows, kv_local, share_count, head_size)
    delta_rows = jnp.sum(
        grad_four.astype(jnp.float32) * attended_heads.astype(jnp.float32), axis=-1
    ).transpose(1, 2, 0)
    back_state = (
        jnp.zeros((group_rows, kv_local, share_count, head_size), jnp.float32),
        jnp.zeros((blocks * group_rows, kv_local * head_size), jnp.float32),
        jnp.zeros((blocks * group_rows, kv_local * head_size), jnp.float32),
    )
    key_piece = lax.all_gather(k_heads, "blk", axis=0, tiled=True)
    value_piece = lax.all_gather(v_heads, "blk", axis=0, tiled=True)
    row_count = key_piece.shape[0]
    collect_key_three = key_piece.reshape(row_count, kv_local, head_size)
    collect_value_three = value_piece.reshape(row_count, kv_local, head_size)
    collect_causal = key_where(row_count)[None, :] <= query_where[:, None]

    def update(held_state):
        scores = (
            jnp.einsum(
                "qkgd,nkd->kgqn", q_four, collect_key_three, preferred_element_type=jnp.float32
            )
            * score_scale
        )
        scores = jnp.where(collect_causal, scores, NEG)
        prob_rows = jnp.where(collect_causal, jnp.exp(scores - log_total[..., None]), 0.0)
        value_part = jnp.einsum(
            "kgqn,qkgd->nkd",
            prob_rows.astype(jnp.bfloat16),
            grad_four,
            preferred_element_type=jnp.float32,
        )
        dprob = jnp.einsum(
            "qkgd,nkd->kgqn", grad_four, collect_value_three, preferred_element_type=jnp.float32
        )
        dscore = (prob_rows * (dprob - delta_rows[..., None])).astype(jnp.bfloat16)
        query_acc = (
            jnp.einsum(
                "kgqn,nkd->qkgd", dscore, collect_key_three, preferred_element_type=jnp.float32
            )
            * score_scale
        )
        key_part = (
            jnp.einsum("kgqn,qkgd->nkd", dscore, q_four, preferred_element_type=jnp.float32)
            * score_scale
        )
        key_acc = key_part.reshape(row_count, -1)
        value_acc = value_part.reshape(row_count, -1)
        return (query_acc, key_acc, value_acc)

    query_acc, key_acc, value_acc = update(back_state)
    key_sums, value_sums = (
        lax.psum_scatter(
            key_acc.astype(jnp.bfloat16), "blk", scatter_dimension=0, tiled=True
        ).astype(jnp.float32),
        lax.psum_scatter(
            value_acc.astype(jnp.bfloat16), "blk", scatter_dimension=0, tiled=True
        ).astype(jnp.float32),
    )
    dqueries, dkeys, dvalues = (
        lax.all_to_all(
            query_acc.reshape(group_rows, -1).astype(jnp.bfloat16),
            "head",
            split_axis=0,
            concat_axis=1,
            tiled=True,
        ),
        lax.all_to_all(
            key_sums.astype(jnp.bfloat16), "head", split_axis=0, concat_axis=1, tiled=True
        ),
        lax.all_to_all(
            value_sums.astype(jnp.bfloat16), "head", split_axis=0, concat_axis=1, tiled=True
        ),
    )
    _, query_back = jax.vjp(query_map, q_raw, qk_gain[0])
    dq_raw, qgain_grad = query_back(dqueries.astype(jnp.float32))
    _, key_back = jax.vjp(query_map, k_raw, qk_gain[1])
    dk_raw, kgain_grad = key_back(dkeys.astype(jnp.float32))
    dq_raw = dq_raw.astype(jnp.bfloat16)
    dk_raw = dk_raw.astype(jnp.bfloat16)
    dnormed = jnp.dot(dq_raw, query_full.T, preferred_element_type=jnp.float32)
    dnormed = dnormed + jnp.dot(dk_raw, key_full.T, preferred_element_type=jnp.float32)
    dnormed = dnormed + jnp.dot(dvalues, value_full.T, preferred_element_type=jnp.float32)
    query_grad = jnp.dot(normed.T, dq_raw, preferred_element_type=jnp.float32)
    key_grad = jnp.dot(normed.T, dk_raw, preferred_element_type=jnp.float32)
    value_grad = jnp.dot(normed.T, dvalues, preferred_element_type=jnp.float32)
    _, norm1_back = jax.vjp(rms_norm, in_flat, gain_one)
    dinput_norm, norm1_grad = norm1_back(dnormed)
    input_grad = (dmiddle + dinput_norm).astype(jnp.bfloat16)
    summed = (
        lax.psum_scatter(norm1_grad, ("head", "blk"), scatter_dimension=0, tiled=True),
        lax.psum_scatter(query_grad, ("head", "blk"), scatter_dimension=0, tiled=True),
        lax.psum_scatter(key_grad, ("head", "blk"), scatter_dimension=0, tiled=True),
        lax.psum_scatter(value_grad, ("head", "blk"), scatter_dimension=0, tiled=True),
        lax.psum_scatter(out_proj_grad, ("head", "blk"), scatter_dimension=0, tiled=True),
        lax.psum_scatter(norm2_grad, ("head", "blk"), scatter_dimension=0, tiled=True),
        lax.psum_scatter(gate_grad, ("head", "blk"), scatter_dimension=0, tiled=True),
        lax.psum_scatter(up_grad, ("head", "blk"), scatter_dimension=0, tiled=True),
        lax.psum_scatter(down_grad, ("head", "blk"), scatter_dimension=0, tiled=True),
    )
    qk_gain_grad = lax.psum(jnp.stack([qgain_grad, kgain_grad]), ("head", "blk"))
    return (
        block_output,
        input_grad,
        summed[0],
        summed[1],
        summed[2],
        summed[3],
        qk_gain_grad,
        summed[4],
        summed[5],
        summed[6],
        summed[7],
        summed[8],
    )


def solution(mesh):
    in_specs = (
        P(("head", "blk"), None),
        P(),
        P(("head", "blk")),
        P(("head", "blk"), None),
        P(("head", "blk"), None),
        P(("head", "blk"), None),
        P(),
        P(("head", "blk"), None),
        P(("head", "blk")),
        P(("head", "blk"), None),
        P(("head", "blk"), None),
        P(("head", "blk"), None),
        P(("head", "blk"), None),
    )
    out_specs = (
        P(("head", "blk"), None),
        P(("head", "blk"), None),
        P(("head", "blk")),
        P(("head", "blk"), None),
        P(("head", "blk"), None),
        P(("head", "blk"), None),
        P(),
        P(("head", "blk"), None),
        P(("head", "blk")),
        P(("head", "blk"), None),
        P(("head", "blk"), None),
        P(("head", "blk"), None),
    )
    return jax.shard_map(local, mesh=mesh, in_specs=in_specs, out_specs=out_specs, check_vma=False)
```

profile of v0, /device:TPU:0, one launch (start us, length us, event | category | flops | bytes accessed | tf_op | source)
XLA Modules:
  0.0 1968.1 jit_solution(9084363389160186047)
XLA Ops:
  11.1 42.0 %all-reduce.9 = (bf16[1024]{0:T(1024)(128)(2,1)S(1)}, bf16[1024]{0:T(1024)(128)(2,1)S(1)}) all-reduce(bf16[1024]{0:T(1024)(128)(2,1)S(1)} %dynamic-update-slice, bf16[1024]{0:T(1024)(128)(2,1)S(1)} %dynamic-update-slice.1), channel_id=1, replica_groups=mesh['head'=4,'blk'=8] {'head','blk'}, use_global_device_ids=true, to_apply=%add.4 | all-reduce | flops 2048 | bytes 8192
  54.9 12.6 all-gather.10.cloned.1.call-done
  69.9 3.3 all-to-all-start
  73.3 4.5 all-to-all-done
  79.5 43.9 %all-gather.14.cloned.1.call-done = bf16[1024,512]{1,0:T(8,128)(2,1)} async-done(((bf16[32,512]{1,0:T(8,128)(2,1)}), bf16[1024,512]{1,0:T(8,128)(2,1)}) %all-gather.14.cloned.1.call-update) | async-done | bytes 1048592 | tf_op jit(solution)/shard_map/all_gather | solution.py:93
  126.2 7.1 all_to_all.125
  138.5 43.2 %all-gather.18.cloned.1.call-done = bf16[1024,1024]{1,0:T(8,128)(2,1)} async-done(((bf16[32,1024]{1,0:T(8,128)(2,1)}), bf16[1024,1024]{1,0:T(8,128)(2,1)}) %all-gather.18.cloned.1.call-update) | async-done | bytes 2097168 | tf_op jit(solution)/shard_map/all_gather | solution.py:92
  185.4 3.7 all-to-all-start.2
  191.4 32.0 %all-gather.12.cloned.1.call-done = bf16[4096,128]{1,0:T(8,128)(2,1)} async-done(((bf16[512,128]{1,0:T(8,128)(2,1)}), bf16[4096,128]{1,0:T(8,128)(2,1)}) %all-gather.12.cloned.1.call-update) | async-done | bytes 1048592 | tf_op jit(solution)/shard_map/all_gather | solution.py:144
  225.8 39.3 %all-gather.16.cloned.1.call-done = bf16[4096,128]{1,0:T(8,128)(2,1)} async-done(((bf16[512,128]{1,0:T(8,128)(2,1)}), bf16[4096,128]{1,0:T(8,128)(2,1)}) %all-gather.16.cloned.1.call-update) | async-done | bytes 1048592 | tf_op jit(solution)/shard_map/all_gather | solution.py:143
  266.9 15.1 fusion.5
  282.1 15.2 fusion.2
  297.3 15.4 fusion.34
  313.6 3.9 all-to-all-start.3
  317.5 5.5 all-gather.20.cloned.1.call-done
  325.9 80.5 %all-gather.24.cloned.1.call-done = bf16[1024,4608]{1,0:T(8,128)(2,1)} async-done(((bf16[32,4608]{1,0:T(8,128)(2,1)}), bf16[1024,4608]{1,0:T(8,128)(2,1)}) %all-gather.24.cloned.1.call-update) | async-done | bytes 9437200 | tf_op jit(solution)/shard_map/all_gather | solution.py:98
  406.4 6.5 fusion.101
  412.9 76.5 %all-gather.22.cloned.1.call-done = bf16[1024,4608]{1,0:T(8,128)(2,1)} async-done(((bf16[32,4608]{1,0:T(8,128)(2,1)}), bf16[1024,4608]{1,0:T(8,128)(2,1)}) %all-gather.22.cloned.1.call-update) | async-done | bytes 9437200 | tf_op jit(solution)/shard_map/all_gather | solution.py:97
  489.4 6.5 fusion.100
  495.9 76.5 %all-gather.26.cloned.1.call-done = bf16[4608,1024]{1,0:T(8,128)(2,1)} async-done(((bf16[144,1024]{1,0:T(8,128)(2,1)}), bf16[4608,1024]{1,0:T(8,128)(2,1)}) %all-gather.26.cloned.1.call-update) | async-done | bytes 9437200 | tf_op jit(solution)/shard_map/all_gather | solution.py:99
  572.4 9.0 multiply_convert_fusion
  581.5 3.1 fusion.102
  584.6 7.6 multiply_reduce_fusion
  594.8 3.4 all-to-all-start.4
  599.8 4.4 all-to-all-done.4
  607.9 15.8 fusion.16
  626.1 23.3 %fusion.1 = bf16[2,2,512,4096]{2,3,1,0:T(8,128)(2,1)} fusion(f32[2,4096,512,2]{2,1,3,0:T(8,128)} %get-tuple-element.45, f32[2,2,512]{2,1,0:T(2,128)} %bitcast.199, f32[2,2,512]{2,1,0:T(2,128)} %log_add_fusion, pred[512,4096]{0,1:T(8,128)(4,1)} %broadcast_compare_fusion, bf16[4096,2,64,1]{0,2,3,1:T(8,128)(2,1)} %bitcast.184, ...), kind=kOutput, calls=%fused_computation.2 | convolution fusion | flops 1132462080 | bytes 53755904 | tf_op jit(solution)/shard_map/qkgd,nkd->kgqn/dot_general | solution.py:258
  649.4 12.0 fusion.19
  663.8 25.1 %reduce-scatter.12.cloned.1.call-done = bf16[512,128]{1,0:T(8,128)(2,1)} async-done(((bf16[4096,128]{1,0:T(8,128)(2,1)}), bf16[512,128]{1,0:T(8,128)(2,1)}) %reduce-scatter.12.cloned.1.call-update) | async-done | bytes 131088 | tf_op jit(solution)/shard_map/reduce_scatter | solution.py:281
  688.8 8.6 all_to_all.126
  702.0 53.6 %reduce-scatter.10.cloned.1.call-done = bf16[512,128]{1,0:T(8,128)(2,1)} async-done(((bf16[4096,128]{1,0:T(8,128)(2,1)}), bf16[512,128]{1,0:T(8,128)(2,1)}) %reduce-scatter.10.cloned.1.call-update) | async-done | bytes 131088 | tf_op jit(solution)/shard_map/reduce_scatter | solution.py:278
  755.6 7.9 all_to_all.127
  773.6 3.6 fusion.48
  777.3 9.1 fusion.29
  788.1 9.1 all_to_all.128
  800.7 3.4 fusion.93
  804.2 8.9 fusion.106
  813.1 9.2 fusion.105
  822.4 9.1 fusion.104
  831.6 5.9 fusion.27
  839.6 39.0 %all-reduce.8 = (f32[1024]{0:T(1024)S(1)}, f32[2,64]{1,0:T(2,128)}, f32[1024]{0:T(1024)S(1)}) all-reduce(f32[1024]{0:T(1024)S(1)} %get-tuple-element.14, f32[2,64]{1,0:T(2,128)S(1)} %pad_maximum_fusion.2, f32[1024]{0:T(1024)S(1)} %copy-done.36), channel_id=4, replica_groups=mesh['head'=4,'blk'=8] {'head','blk'}, use_global_device_ids=true, to_apply=%region_17.18.clone | all-reduce | flops 2176 | bytes 17408
  881.3 15.1 reduce-scatter.18.cloned.1.call-done
  896.4 138.7 %reduce-scatter.16.cloned.1.call-done = f32[32,512]{1,0:T(8,128)} async-done(((f32[1024,512]{1,0:T(8,128)}), f32[32,512]{1,0:T(8,128)}) %reduce-scatter.16.cloned.1.call-update) | async-done | bytes 65552 | tf_op jit(solution)/shard_map/reduce_scatter | solution.py:318
  1035.1 143.4 %reduce-scatter.20.cloned.1.call-done = f32[32,1024]{1,0:T(8,128)} async-done(((f32[1024,1024]{1,0:T(8,128)}), f32[32,1024]{1,0:T(8,128)}) %reduce-scatter.20.cloned.1.call-update) | async-done | bytes 131088 | tf_op jit(solution)/shard_map/reduce_scatter | solution.py:320
  1178.5 145.4 %reduce-scatter.14.cloned.1.call-done = f32[32,1024]{1,0:T(8,128)} async-done(((f32[1024,1024]{1,0:T(8,128)}), f32[32,1024]{1,0:T(8,128)}) %reduce-scatter.14.cloned.1.call-update) | async-done | bytes 131088 | tf_op jit(solution)/shard_map/reduce_scatter | solution.py:317
  1323.9 211.1 %reduce-scatter.26.cloned.1.call-done = f32[144,1024]{1,0:T(8,128)} async-done(((f32[4608,1024]{1,0:T(8,128)}), f32[144,1024]{1,0:T(8,128)}) %reduce-scatter.26.cloned.1.call-update) | async-done | bytes 589840 | tf_op jit(solution)/shard_map/reduce_scatter | solution.py:324
  1535.0 213.0 %reduce-scatter.24.cloned.1.call-done = f32[32,4608]{1,0:T(8,128)} async-done(((f32[1024,4608]{1,0:T(8,128)}), f32[32,4608]{1,0:T(8,128)}) %reduce-scatter.24.cloned.1.call-update) | async-done | bytes 589840 | tf_op jit(solution)/shard_map/reduce_scatter | solution.py:323
  1748.0 213.0 %reduce-scatter.22.cloned.1.call-done = f32[32,4608]{1,0:T(8,128)} async-done(((f32[1024,4608]{1,0:T(8,128)}), f32[32,4608]{1,0:T(8,128)}) %reduce-scatter.22.cloned.1.call-update) | async-done | bytes 589840 | tf_op jit(solution)/shard_map/reduce_scatter | solution.py:322
  (200 shorter events, 68.5 us)
Async XLA Ops:
  7.2 60.4 %all-gather.10.cloned.1.call-start = ((), (), s32[]{:S(2)}) async-start(), calls=%async_computation.17 | async-start | bytes 1081344 | tf_op jit(solution)/shard_map/all_gather | solution.py:94
  7.9 115.4 %all-gather.14.cloned.1.call-start = ((), (), s32[]{:S(2)}) async-start(), calls=%async_computation.19 | async-start | bytes 1081344 | tf_op jit(solution)/shard_map/all_gather | solution.py:93
  8.7 173.1 %all-gather.18.cloned.1.call-start = ((), (), s32[]{:S(2)}) async-start(), calls=%async_computation.21 | async-start | bytes 2162688 | tf_op jit(solution)/shard_map/all_gather | solution.py:92
  53.1 132.3 %copy-start.25 = (f32[1024]{0:T(1024)}, f32[1024]{0:T(1024)S(1)}, u32[]{:S(2)}) copy-start(f32[1024]{0:T(1024)S(1)} %convert_element_type.147) | copy-start | bytes 12292
  54.9 24.5 %copy-start.41 = (f32[128]{0:T(128)}, f32[128]{0:T(128)S(1)}, u32[]{:S(2)}) copy-start(f32[128]{0:T(128)S(1)} %fusion.45) | copy-start | bytes 1540
  54.9 211.6 %copy-start.33 = (f32[128]{0:T(128)}, f32[128]{0:T(128)S(1)}, u32[]{:S(2)}) copy-start(f32[128]{0:T(128)S(1)} %fusion.81) | copy-start | bytes 1540
  69.9 7.9 all-to-all-start
  73.2 150.2 %all-gather.12.cloned.1.call-start = ((), (), s32[]{:S(2)}) async-start(), calls=%async_computation.18 | async-start | bytes 1179648 | tf_op jit(solution)/shard_map/all_gather | solution.py:144
  78.5 186.5 %all-gather.16.cloned.1.call-start = ((), (), s32[]{:S(2)}) async-start(), calls=%async_computation.20 | async-start | bytes 1179648 | tf_op jit(solution)/shard_map/all_gather | solution.py:143
  79.3 187.2 %copy-start.37 = (f32[64]{0:T(128)}, f32[64]{0:T(128)S(1)}, u32[]{:S(2)}) copy-start(f32[64]{0:T(128)S(1)} %get-tuple-element.36) | copy-start | bytes 772
  79.3 187.2 %copy-start.38 = (f32[64]{0:T(128)}, f32[64]{0:T(128)S(1)}, u32[]{:S(2)}) copy-start(f32[64]{0:T(128)S(1)} %get-tuple-element.37) | copy-start | bytes 772
  79.5 105.9 %copy-start.24 = (f32[128,32]{0,1:T(8,128)}, f32[128,32]{0,1:T(8,128)S(1)}, u32[]{:S(2)}) copy-start(f32[128,32]{0,1:T(8,128)S(1)} %get-tuple-element.39) | copy-start | bytes 49156
  134.1 188.9 %all-gather.20.cloned.1.call-start = ((), (), s32[]{:S(2)}) async-start(), calls=%async_computation.22 | async-start | bytes 2162688 | tf_op jit(solution)/shard_map/all_gather | solution.py:95
  134.7 271.7 %all-gather.24.cloned.1.call-start = ((), (), s32[]{:S(2)}) async-start(), calls=%async_computation.24 | async-start | bytes 9732096 | tf_op jit(solution)/shard_map/all_gather | solution.py:98
  135.4 354.0 %all-gather.22.cloned.1.call-start = ((), (), s32[]{:S(2)}) async-start(), calls=%async_computation.23 | async-start | bytes 9732096 | tf_op jit(solution)/shard_map/all_gather | solution.py:97
  136.2 436.3 %all-gather.26.cloned.1.call-start = ((), (), s32[]{:S(2)}) async-start(), calls=%async_computation.25 | async-start | bytes 9732096 | tf_op jit(solution)/shard_map/all_gather | solution.py:99
  185.4 81.1 %all-to-all-start.2 = ((bf16[128,4,256]{0,2,1:T(8,128)(2,1)}), bf16[128,4,256]{0,2,1:T(8,128)(2,1)S(1)}, u32[]{:S(2)}, u32[]{:S(2)}) async-start(bf16[128,4,256]{0,2,1:T(8,128)(2,1)} %bitcast.15), calls=%async_computation.2 | async-start | bytes 524288 | tf_op jit(solution)/shard_map/all_to_all | solution.py:127
  266.5 15.5 copy-start.2
  266.9 15.1 copy-start.13
  266.9 15.1 copy-start.3
  282.0 15.3 copy-start.32
  282.0 15.2 copy-start.4
  282.1 15.2 copy-start.20
  297.3 15.5 copy-start.35
  297.3 26.2 %copy-start.1 = (bf16[128,1024]{1,0:T(8,128)(2,1)S(1)}, bf16[128,1024]{1,0:T(8,128)(2,1)}, u32[]{:S(2)}) copy-start(bf16[128,1024]{1,0:T(8,128)(2,1)} %param.13) | copy-start | bytes 786436
  312.8 10.7 copy-start.21
  313.6 9.9 all-to-all-start.3
  317.5 267.0 %copy-start.30 = (f32[1024]{0:T(1024)}, f32[1024]{0:T(1024)S(1)}, u32[]{:S(2)}) copy-start(f32[1024]{0:T(1024)S(1)} %convert_element_type.155) | copy-start | bytes 12292
  323.5 89.4 %copy-start.15 = (bf16[4,128,256]{1,2,0:T(8,128)(2,1)}, bf16[4,128,256]{1,2,0:T(8,128)(2,1)S(1)}, u32[]{:S(2)}) copy-start(bf16[4,128,256]{1,2,0:T(8,128)(2,1)S(1)} %all-to-all-done.3) | copy-start | bytes 786436
  325.7 258.8 %copy-start.39 = (f32[128]{0:T(128)}, f32[128]{0:T(128)S(1)}, u32[]{:S(2)}) copy-start(f32[128]{0:T(128)S(1)} %fusion.82) | copy-start | bytes 1540
  412.9 159.5 %copy-start.19 = (bf16[128,1024]{1,0:T(8,128)(2,1)S(1)}, bf16[128,1024]{1,0:T(8,128)(2,1)}, u32[]{:S(2)}) copy-start(bf16[128,1024]{1,0:T(8,128)(2,1)} %param.25) | copy-start | bytes 786436
  572.4 9.0 copy-start
  581.4 10.8 copy-start.9
  581.4 10.8 copy-start.10
  584.5 8.6 copy-start.6
  594.8 9.4 all-to-all-start.4
  598.2 90.6 %reduce-scatter.12.cloned.1.call-start = ((), (), s32[]{:S(2)}) async-start(), calls=%async_computation.27 | async-start | bytes 1179648 | tf_op jit(solution)/shard_map/reduce_scatter | solution.py:281
  606.2 17.6 copy-start.22
  626.0 129.6 %reduce-scatter.10.cloned.1.call-start = ((), (), s32[]{:S(2)}) async-start(), calls=%async_computation.26 | async-start | bytes 1179648 | tf_op jit(solution)/shard_map/reduce_scatter | solution.py:278
  626.1 23.3 %copy-start.14 = (bf16[512,2,2,64]{0,3,2,1:T(8,128)(2,1)S(1)}, bf16[512,2,2,64]{0,3,2,1:T(8,128)(2,1)}, u32[]{:S(2)}) copy-start(bf16[512,2,2,64]{0,3,2,1:T(8,128)(2,1)} %copy-done.13) | copy-start | bytes 786436
  661.4 105.6 %copy-start.8 = (f32[128,512]{0,1:T(8,128)S(1)}, f32[128,512]{0,1:T(8,128)}, u32[]{:S(2)}) copy-start(f32[128,512]{0,1:T(8,128)} %copy-done.7) | copy-start | bytes 786436
  663.7 232.7 %reduce-scatter.18.cloned.1.call-start = ((), (), s32[]{:S(2)}) async-start(), calls=%async_computation.30 | async-start | bytes 2162688 | tf_op jit(solution)/shard_map/reduce_scatter | solution.py:319
  701.9 333.2 %reduce-scatter.16.cloned.1.call-start = ((), (), s32[]{:S(2)}) async-start(), calls=%async_computation.29 | async-start | bytes 2162688 | tf_op jit(solution)/shard_map/reduce_scatter | solution.py:318
  773.3 405.2 %reduce-scatter.20.cloned.1.call-start = ((), (), s32[]{:S(2)}) async-start(), calls=%async_computation.31 | async-start | bytes 4325376 | tf_op jit(solution)/shard_map/reduce_scatter | solution.py:320
  777.2 546.7 %reduce-scatter.14.cloned.1.call-start = ((), (), s32[]{:S(2)}) async-start(), calls=%async_computation.28 | async-start | bytes 4325376 | tf_op jit(solution)/shard_map/reduce_scatter | solution.py:317
  804.1 730.9 %reduce-scatter.26.cloned.1.call-start = ((), (), s32[]{:S(2)}) async-start(), calls=%async_computation.34 | async-start | bytes 19464192 | tf_op jit(solution)/shard_map/reduce_scatter | solution.py:324
  813.1 935.0 %reduce-scatter.24.cloned.1.call-start = ((), (), s32[]{:S(2)}) async-start(), calls=%async_computation.33 | async-start | bytes 19464192 | tf_op jit(solution)/shard_map/reduce_scatter | solution.py:323
  822.3 1138.7 %reduce-scatter.22.cloned.1.call-start = ((), (), s32[]{:S(2)}) async-start(), calls=%async_computation.32 | async-start | bytes 19464192 | tf_op jit(solution)/shard_map/reduce_scatter | solution.py:322
  (16 other events, 76.9 us)
Sparse Core Ops, SparseCore 0:
  11.0 56.5 all-gather.9
  70.5 52.7 all-gather.13
  126.3 55.3 all-gather.17
  184.3 39.1 all-gather.11
  226.0 38.9 all-gather.15
  267.9 55.1 all-gather.19
  326.0 80.3 all-gather.23
  409.3 80.0 all-gather.21
  492.4 80.0 all-gather.25
  626.2 62.6 reduce-scatter.11
  692.2 63.3 reduce-scatter.9
  758.3 138.0 reduce-scatter.17
  899.2 135.7 reduce-scatter.15
  1037.8 140.6 reduce-scatter.19
  1181.2 142.6 reduce-scatter.13
  1330.8 204.2 reduce-scatter.25
  1541.9 206.1 reduce-scatter.23
  1754.9 206.0 reduce-scatter.21
where the time goes:
time: 1970 us
  waiting for transfers between devices  1580 us (80%)
  matrix products  180 us (9%)
  blocking collectives  114 us (6%)
  other arithmetic  35.8 us (2%)
  local copies, waits for them, and re-layouts  24.7 us (1%)
    reduce_scatter x1, waiting for transfers between devices, local(): lax.psum_scatter(up_grad, ('head', 'blk'), scatter_dimension=0, tiled=True)  213 us
    reduce_scatter x1, waiting for transfers between devices, local(): lax.psum_scatter(gate_grad, ('head', 'blk'), scatter_dimension=0, tiled=T...  213 us
    reduce_scatter x1, waiting for transfers between devices, local(): lax.psum_scatter(down_grad, ('head', 'blk'), scatter_dimension=0, tiled=T...  211 us
    reduce_scatter x1, waiting for transfers between devices, local(): lax.psum_scatter(query_grad, ('head', 'blk'), scatter_dimension=0, tiled=...  145 us
    reduce_scatter x1, waiting for transfers between devices, local(): lax.psum_scatter(out_proj_grad, ('head', 'blk'), scatter_dimension=0, til...  143 us
    reduce_scatter x1, waiting for transfers between devices, local(): lax.psum_scatter(key_grad, ('head', 'blk'), scatter_dimension=0, tiled=True)  139 us
    unnamed x2, blocking collectives  81 us
    all_gather x1, waiting for transfers between devices, local(): lax.all_gather(w_up, ('head', 'blk'), axis=0, tiled=True)  80.5 us
  transfers between devices with their start and end apart: 22, of which 21 were waited for; matrix products, arithmetic and copies ran while one was open for 10% of the time, Pallas kernels for 0%

commit v1 on v0

--- a/solution.py
+++ b/solution.py
@@ -140,8 +140,11 @@
         jnp.zeros((kv_local, share_count, group_rows), jnp.float32),
         jnp.zeros((group_rows, kv_local, share_count, head_size), jnp.float32),
     )
-    key_piece = lax.all_gather(k_heads, "blk", axis=0, tiled=True)
-    value_piece = lax.all_gather(v_heads, "blk", axis=0, tiled=True)
+    key_piece, value_piece = jnp.split(
+        lax.all_gather(jnp.concatenate([k_heads, v_heads], axis=1), "blk", axis=0, tiled=True),
+        [k_heads.shape[1]],
+        axis=1,
+    )
     row_count = key_piece.shape[0]
     key_three = key_piece.reshape(row_count, kv_local, head_size)
     value_three = value_piece.reshape(row_count, kv_local, head_size)

time: 1970 us -> 2050 us (1.041)
  waiting for transfers between devices: 1580 us -> 1620 us
    reduce_scatter x1, waiting for transfers between devices: 15.1 us -> 139 us  [local(): lax.psum_scatter(value_grad, ('head', 'blk'), scatter_dimension=0, tiled=...]
    reduce_scatter x1, waiting for transfers between devices: 139 us -> 20.6 us  [local(): lax.psum_scatter(key_grad, ('head', 'blk'), scatter_dimension=0, tiled=True)]
    all_gather x0 -> x1, waiting for transfers between devices: none -> 46 us  [local(): lax.all_gather(jnp.concatenate([k_heads, v_heads], axis=1), 'blk', axis=0...]
    all_gather x1, waiting for transfers between devices: 43.9 us -> 11.1 us  [local(): lax.all_gather(key_weight, ('head', 'blk'), axis=0, tiled=True)]
    all_gather x1, waiting for transfers between devices: 12.6 us -> 45 us  [local(): lax.all_gather(value_weight, ('head', 'blk'), axis=0, tiled=True)]
    reduce_scatter x1, waiting for transfers between devices: 25.1 us -> 48.2 us  [local(): lax.psum_scatter(value_acc.astype(jnp.bfloat16), 'blk', scatter_dimension...]
  transfers between devices with their start and end apart: 22 -> 22, of which waited for: 21 -> 19; matrix products, arithmetic and copies ran while one was open for 10% -> 10% of each run, Pallas kernels for 0% -> 0%
where the time goes in v1:
time: 2050 us; the launch traced here: 2040 us
  waiting for transfers between devices  1620 us (79%)
  matrix products  197 us (10%)
  blocking collectives  121 us (6%)
  local copies, waits for them, and re-layouts  37.8 us (2%)
  other arithmetic  37 us (2%)
    reduce_scatter x1, waiting for transfers between devices, local(): lax.psum_scatter(down_grad, ('head', 'blk'), scatter_dimension=0, tiled=T...  213 us
    reduce_scatter x1, waiting for transfers between devices, local(): lax.psum_scatter(up_grad, ('head', 'blk'), scatter_dimension=0, tiled=True)  213 us
    reduce_scatter x1, waiting for transfers between devices, local(): lax.psum_scatter(gate_grad, ('head', 'blk'), scatter_dimension=0, tiled=T...  211 us
    reduce_scatter x1, waiting for transfers between devices, local(): lax.psum_scatter(query_grad, ('head', 'blk'), scatter_dimension=0, tiled=...  145 us
    reduce_scatter x1, waiting for transfers between devices, local(): lax.psum_scatter(out_proj_grad, ('head', 'blk'), scatter_dimension=0, til...  144 us
    reduce_scatter x1, waiting for transfers between devices, local(): lax.psum_scatter(value_grad, ('head', 'blk'), scatter_dimension=0, tiled=...  139 us
    unnamed x2, blocking collectives  81.1 us
    all_gather x1, waiting for transfers between devices, local(): lax.all_gather(w_up, ('head', 'blk'), axis=0, tiled=True)  76.5 us
  transfers between devices with their start and end apart: 22, of which 19 were waited for; matrix products, arithmetic and copies ran while one was open for 10% of the time, Pallas kernels for 0%

profile of v1, /device:TPU:0, one launch (start us, length us, event | category | flops | bytes accessed | tf_op | source)
XLA Modules:
  0.0 2041.4 jit_solution(6530560837728702071)
XLA Ops:
  11.1 42.0 %all-reduce.9 = (bf16[1024]{0:T(1024)(128)(2,1)S(1)}, bf16[1024]{0:T(1024)(128)(2,1)S(1)}) all-reduce(bf16[1024]{0:T(1024)(128)(2,1)S(1)} %dynamic-update-slice, bf16[1024]{0:T(1024)(128)(2,1)S(1)} %dynamic-update-slice.1), channel_id=1, replica_groups=mesh['head'=4,'blk'=8] {'head','blk'}, use_global_device_ids=true, to_apply=%add.4 | all-reduce | flops 2048 | bytes 8192
  56.5 11.1 all-gather.11.cloned.1.call-done
  70.3 7.1 all_to_all.125
  78.3 45.0 %all-gather.13.cloned.1.call-done = bf16[1024,512]{1,0:T(8,128)(2,1)} async-done(((bf16[32,512]{1,0:T(8,128)(2,1)}), bf16[1024,512]{1,0:T(8,128)(2,1)}) %all-gather.13.cloned.1.call-update) | async-done | bytes 1048592 | tf_op jit(solution)/shard_map/all_gather | solution.py:94
  125.0 7.7 all_to_all.126
  139.0 42.8 %all-gather.17.cloned.1.call-done = bf16[1024,1024]{1,0:T(8,128)(2,1)} async-done(((bf16[32,1024]{1,0:T(8,128)(2,1)}), bf16[1024,1024]{1,0:T(8,128)(2,1)}) %all-gather.17.cloned.1.call-update) | async-done | bytes 2097168 | tf_op jit(solution)/shard_map/all_gather | solution.py:92
  186.2 3.9 all-to-all-start.2
  192.1 31.4 %all-gather.27.cloned.1.call-done = bf16[4096,128]{1,0:T(8,128)(2,1)} async-done(((bf16[512,128]{1,0:T(8,128)(2,1)}), bf16[4096,128]{1,0:T(8,128)(2,1)}) %all-gather.27.cloned.1.call-update) | async-done | bytes 1048592 | tf_op jit(solution)/shard_map/all_gather | solution.py:239
  224.9 39.5 %all-gather.29.cloned.1.call-done = bf16[4096,128]{1,0:T(8,128)(2,1)} async-done(((bf16[512,128]{1,0:T(8,128)(2,1)}), bf16[4096,128]{1,0:T(8,128)(2,1)}) %all-gather.29.cloned.1.call-update) | async-done | bytes 1048592 | tf_op jit(solution)/shard_map/all_gather | solution.py:240
  268.8 46.0 %all-gather.15.cloned.1.call-done = bf16[4096,256]{1,0:T(8,128)(2,1)} async-done(((bf16[512,256]{1,0:T(8,128)(2,1)}), bf16[4096,256]{1,0:T(8,128)(2,1)}) %all-gather.15.cloned.1.call-update) | async-done | bytes 2097168 | tf_op jit(solution)/shard_map/all_gather | solution.py:144
  322.5 14.9 fusion.5
  337.4 15.1 fusion.6
  352.6 15.2 fusion.37
  368.6 3.6 all-to-all-start.3
  372.2 14.5 fusion.107
  389.1 67.1 %all-gather.21.cloned.1.call-done = bf16[1024,4608]{1,0:T(8,128)(2,1)} async-done(((bf16[32,4608]{1,0:T(8,128)(2,1)}), bf16[1024,4608]{1,0:T(8,128)(2,1)}) %all-gather.21.cloned.1.call-update) | async-done | bytes 9437200 | tf_op jit(solution)/shard_map/all_gather | solution.py:97
  456.2 6.6 fusion.104
  462.7 76.5 %all-gather.23.cloned.1.call-done = bf16[1024,4608]{1,0:T(8,128)(2,1)} async-done(((bf16[32,4608]{1,0:T(8,128)(2,1)}), bf16[1024,4608]{1,0:T(8,128)(2,1)}) %all-gather.23.cloned.1.call-update) | async-done | bytes 9437200 | tf_op jit(solution)/shard_map/all_gather | solution.py:98
  539.2 6.5 fusion.105
  545.8 76.3 %all-gather.25.cloned.1.call-done = bf16[4608,1024]{1,0:T(8,128)(2,1)} async-done(((bf16[144,1024]{1,0:T(8,128)(2,1)}), bf16[4608,1024]{1,0:T(8,128)(2,1)}) %all-gather.25.cloned.1.call-update) | async-done | bytes 9437200 | tf_op jit(solution)/shard_map/all_gather | solution.py:99
  622.1 8.8 multiply_convert_fusion
  632.0 7.7 fusion.106
  639.7 3.8 multiply_reduce_fusion
  647.0 4.3 all-to-all-start.4
  652.6 4.7 all-to-all-done.4
  662.6 23.3 %fusion.1 = bf16[2,2,512,4096]{2,3,1,0:T(8,128)(2,1)} fusion(f32[2,4096,512,2]{2,1,3,0:T(8,128)} %fusion.107, f32[2,2,512]{2,1,0:T(2,128)} %bitcast.224, f32[2,2,512]{2,1,0:T(2,128)} %log_add_fusion, pred[512,4096]{0,1:T(8,128)(4,1)} %copy-done.6, bf16[4096,2,64,1]{0,2,3,1:T(8,128)(2,1)} %bitcast.210, bf16[512,2,2,64]{0,3,2,1:T(8,128)(2,1)} %reshape.435), kind=kOutput, calls=%fused_computation.2 | convolution fusion | flops 1132462080 | bytes 53755904 | tf_op jit(solution)/shard_map/qkgd,nkd->kgqn/dot_general | solution.py:261
  685.9 12.0 fusion.22
  700.7 17.4 fusion.19
  720.4 42.6 %reduce-scatter.10.cloned.1.call-done = bf16[512,128]{1,0:T(8,128)(2,1)} async-done(((bf16[4096,128]{1,0:T(8,128)(2,1)}), bf16[512,128]{1,0:T(8,128)(2,1)}) %reduce-scatter.10.cloned.1.call-update) | async-done | bytes 131088 | tf_op jit(solution)/shard_map/reduce_scatter | solution.py:281
  763.0 7.9 all_to_all.127
  781.2 48.2 %reduce-scatter.12.cloned.1.call-done = bf16[512,128]{1,0:T(8,128)(2,1)} async-done(((bf16[4096,128]{1,0:T(8,128)(2,1)}), bf16[512,128]{1,0:T(8,128)(2,1)}) %reduce-scatter.12.cloned.1.call-update) | async-done | bytes 131088 | tf_op jit(solution)/shard_map/reduce_scatter | solution.py:284
  829.4 8.6 all_to_all.128
  842.6 3.6 fusion.51
  846.3 9.5 fusion.32
  856.9 8.6 all_to_all.129
  868.9 3.5 fusion.96
  872.6 9.2 fusion.109
  881.9 9.2 fusion.110
  892.1 7.8 fusion.111
  900.1 5.9 fusion.30
  908.1 39.0 %all-reduce.8 = (f32[1024]{0:T(1024)S(1)}, f32[2,64]{1,0:T(2,128)}, f32[1024]{0:T(1024)S(1)}) all-reduce(f32[1024]{0:T(1024)S(1)} %get-tuple-element.14, f32[2,64]{1,0:T(2,128)S(1)} %pad_maximum_fusion.3, f32[1024]{0:T(1024)S(1)} %copy-done.41), channel_id=4, replica_groups=mesh['head'=4,'blk'=8] {'head','blk'}, use_global_device_ids=true, to_apply=%region_17.18.clone | all-reduce | flops 2176 | bytes 17408
  949.8 20.6 %reduce-scatter.16.cloned.1.call-done = f32[32,512]{1,0:T(8,128)} async-done(((f32[1024,512]{1,0:T(8,128)}), f32[32,512]{1,0:T(8,128)}) %reduce-scatter.16.cloned.1.call-update) | async-done | bytes 65552 | tf_op jit(solution)/shard_map/reduce_scatter | solution.py:321
  970.4 138.6 %reduce-scatter.18.cloned.1.call-done = f32[32,512]{1,0:T(8,128)} async-done(((f32[1024,512]{1,0:T(8,128)}), f32[32,512]{1,0:T(8,128)}) %reduce-scatter.18.cloned.1.call-update) | async-done | bytes 65552 | tf_op jit(solution)/shard_map/reduce_scatter | solution.py:322
  1109.0 144.4 %reduce-scatter.20.cloned.1.call-done = f32[32,1024]{1,0:T(8,128)} async-done(((f32[1024,1024]{1,0:T(8,128)}), f32[32,1024]{1,0:T(8,128)}) %reduce-scatter.20.cloned.1.call-update) | async-done | bytes 131088 | tf_op jit(solution)/shard_map/reduce_scatter | solution.py:323
  1253.4 144.9 %reduce-scatter.14.cloned.1.call-done = f32[32,1024]{1,0:T(8,128)} async-done(((f32[1024,1024]{1,0:T(8,128)}), f32[32,1024]{1,0:T(8,128)}) %reduce-scatter.14.cloned.1.call-update) | async-done | bytes 131088 | tf_op jit(solution)/shard_map/reduce_scatter | solution.py:320
  1398.3 210.7 %reduce-scatter.22.cloned.1.call-done = f32[32,4608]{1,0:T(8,128)} async-done(((f32[1024,4608]{1,0:T(8,128)}), f32[32,4608]{1,0:T(8,128)}) %reduce-scatter.22.cloned.1.call-update) | async-done | bytes 589840 | tf_op jit(solution)/shard_map/reduce_scatter | solution.py:325
  1608.9 212.8 %reduce-scatter.24.cloned.1.call-done = f32[32,4608]{1,0:T(8,128)} async-done(((f32[1024,4608]{1,0:T(8,128)}), f32[32,4608]{1,0:T(8,128)}) %reduce-scatter.24.cloned.1.call-update) | async-done | bytes 589840 | tf_op jit(solution)/shard_map/reduce_scatter | solution.py:326
  1821.7 212.9 %reduce-scatter.26.cloned.1.call-done = f32[144,1024]{1,0:T(8,128)} async-done(((f32[4608,1024]{1,0:T(8,128)}), f32[144,1024]{1,0:T(8,128)}) %reduce-scatter.26.cloned.1.call-update) | async-done | bytes 589840 | tf_op jit(solution)/shard_map/reduce_scatter | solution.py:327
  (223 shorter events, 83.2 us)
Async XLA Ops:
  7.2 60.4 %all-gather.11.cloned.1.call-start = ((), (), s32[]{:S(2)}) async-start(), calls=%async_computation.17 | async-start | bytes 1081344 | tf_op jit(solution)/shard_map/all_gather | solution.py:93
  7.9 115.4 %all-gather.13.cloned.1.call-start = ((), (), s32[]{:S(2)}) async-start(), calls=%async_computation.18 | async-start | bytes 1081344 | tf_op jit(solution)/shard_map/all_gather | solution.py:94
  8.7 173.1 %all-gather.17.cloned.1.call-start = ((), (), s32[]{:S(2)}) async-start(), calls=%async_computation.20 | async-start | bytes 2162688 | tf_op jit(solution)/shard_map/all_gather | solution.py:92
  9.4 214.1 %all-gather.27.cloned.1.call-start = ((), (), s32[]{:S(2)}) async-start(), calls=%async_computation.25 | async-start | bytes 1179648 | tf_op jit(solution)/shard_map/all_gather | solution.py:239
  53.2 133.0 %copy-start.29 = (f32[1024]{0:T(1024)}, f32[1024]{0:T(1024)S(1)}, u32[]{:S(2)}) copy-start(f32[1024]{0:T(1024)S(1)} %convert_element_type.147) | copy-start | bytes 12292
  55.6 211.2 %copy-start.38 = (f32[128]{0:T(128)}, f32[128]{0:T(128)S(1)}, u32[]{:S(2)}) copy-start(f32[128]{0:T(128)S(1)} %fusion.84) | copy-start | bytes 1540
  56.3 210.5 %copy-start.42 = (f32[64]{0:T(128)}, f32[64]{0:T(128)S(1)}, u32[]{:S(2)}) copy-start(f32[64]{0:T(128)S(1)} %get-tuple-element.38) | copy-start | bytes 772
  56.3 210.5 %copy-start.43 = (f32[64]{0:T(128)}, f32[64]{0:T(128)S(1)}, u32[]{:S(2)}) copy-start(f32[64]{0:T(128)S(1)} %get-tuple-element.39) | copy-start | bytes 772
  56.5 129.7 %copy-start.28 = (f32[128,32]{0,1:T(8,128)}, f32[128,32]{0,1:T(8,128)S(1)}, u32[]{:S(2)}) copy-start(f32[128,32]{0,1:T(8,128)S(1)} %get-tuple-element.41) | copy-start | bytes 49156
  78.3 186.2 %all-gather.29.cloned.1.call-start = ((), (), s32[]{:S(2)}) async-start(), calls=%async_computation.26 | async-start | bytes 1179648 | tf_op jit(solution)/shard_map/all_gather | solution.py:240
  132.7 182.1 %all-gather.15.cloned.1.call-start = ((), (), s32[]{:S(2)}) async-start(), calls=%async_computation.19 | async-start | bytes 2359296 | tf_op jit(solution)/shard_map/all_gather | solution.py:144
  134.5 252.2 %all-gather.19.cloned.1.call-start = ((), (), s32[]{:S(2)}) async-start(), calls=%async_computation.21 | async-start | bytes 2162688 | tf_op jit(solution)/shard_map/all_gather | solution.py:95
  135.3 320.9 %all-gather.21.cloned.1.call-start = ((), (), s32[]{:S(2)}) async-start(), calls=%async_computation.22 | async-start | bytes 9732096 | tf_op jit(solution)/shard_map/all_gather | solution.py:97
  136.0 403.2 %all-gather.23.cloned.1.call-start = ((), (), s32[]{:S(2)}) async-start(), calls=%async_computation.23 | async-start | bytes 9732096 | tf_op jit(solution)/shard_map/all_gather | solution.py:98
  136.7 485.4 %all-gather.25.cloned.1.call-start = ((), (), s32[]{:S(2)}) async-start(), calls=%async_computation.24 | async-start | bytes 9732096 | tf_op jit(solution)/shard_map/all_gather | solution.py:99
  186.2 80.7 %all-to-all-start.2 = ((bf16[128,4,256]{0,2,1:T(8,128)(2,1)}), bf16[128,4,256]{0,2,1:T(8,128)(2,1)S(1)}, u32[]{:S(2)}, u32[]{:S(2)}) async-start(bf16[128,4,256]{0,2,1:T(8,128)(2,1)} %bitcast.15), calls=%async_computation.2 | async-start | bytes 524288 | tf_op jit(solution)/shard_map/all_to_all | solution.py:127
  192.0 160.5 %copy-start.6 = (pred[512,4096]{0,1:T(8,128)(4,1)}, pred[512,4096]{0,1:T(8,128)(4,1)S(1)}, u32[]{:S(2)}) copy-start(pred[512,4096]{0,1:T(8,128)(4,1)S(1)} %broadcast_compare_fusion) | copy-start | bytes 6291460
  192.1 196.9 %copy-start.34 = (f32[1024]{0:T(1024)}, f32[1024]{0:T(1024)S(1)}, u32[]{:S(2)}) copy-start(f32[1024]{0:T(1024)S(1)} %convert_element_type.155) | copy-start | bytes 12292
  268.8 68.6 %copy-start.14 = (bf16[512,2,2,64]{0,3,2,1:T(8,128)(2,1)}, bf16[512,2,2,64]{0,3,2,1:T(8,128)(2,1)S(1)}, u32[]{:S(2)}) copy-start(bf16[512,2,2,64]{0,3,2,1:T(8,128)(2,1)S(1)} %reshape.432) | copy-start | bytes 786436
  337.4 15.1 copy-start.37
  337.4 15.1 copy-start.26
  352.5 15.2 copy-start.40
  368.6 18.1 all-to-all-start.3
  372.2 14.5 copy-start.1
  389.0 156.8 %copy-start.48 = (f32[128]{0:T(128)}, f32[128]{0:T(128)S(1)}, u32[]{:S(2)}) copy-start(f32[128]{0:T(128)S(1)} %get-tuple-element.48) | copy-start | bytes 1540
  389.0 156.8 %copy-start.44 = (f32[128]{0:T(128)}, f32[128]{0:T(128)S(1)}, u32[]{:S(2)}) copy-start(f32[128]{0:T(128)S(1)} %fusion.85) | copy-start | bytes 1540
  389.1 156.7 %copy-start.4 = (bf16[128,1024]{1,0:T(8,128)(2,1)}, bf16[128,1024]{1,0:T(8,128)(2,1)S(1)}, u32[]{:S(2)}) copy-start(bf16[128,1024]{1,0:T(8,128)(2,1)S(1)} %multiply_convert_fusion.2) | copy-start | bytes 786436
  462.7 159.4 %copy-start.23 = (bf16[128,1024]{1,0:T(8,128)(2,1)S(1)}, bf16[128,1024]{1,0:T(8,128)(2,1)}, u32[]{:S(2)}) copy-start(bf16[128,1024]{1,0:T(8,128)(2,1)} %param.25) | copy-start | bytes 786436
  631.0 12.5 copy-start.12
  631.0 8.7 copy-start
  631.0 8.7 copy-start.35
  632.0 11.5 copy-start.49
  632.0 11.5 copy-start.24
  643.7 199.0 %copy-start.9 = (f32[128,1024]{1,0:T(8,128)}, f32[128,1024]{1,0:T(8,128)S(1)}, u32[]{:S(2)}) copy-start(f32[128,1024]{1,0:T(8,128)S(1)} %fusion.44) | copy-start | bytes 1572868
  647.0 10.3 all-to-all-start.4
  651.2 111.8 %reduce-scatter.10.cloned.1.call-start = ((), (), s32[]{:S(2)}) async-start(), calls=%async_computation.27 | async-start | bytes 1179648 | tf_op jit(solution)/shard_map/reduce_scatter | solution.py:281
  700.2 129.2 %reduce-scatter.12.cloned.1.call-start = ((), (), s32[]{:S(2)}) async-start(), calls=%async_computation.28 | async-start | bytes 1179648 | tf_op jit(solution)/shard_map/reduce_scatter | solution.py:284
  720.3 250.1 %reduce-scatter.16.cloned.1.call-start = ((), (), s32[]{:S(2)}) async-start(), calls=%async_computation.30 | async-start | bytes 2162688 | tf_op jit(solution)/shard_map/reduce_scatter | solution.py:321
  781.2 327.8 %reduce-scatter.18.cloned.1.call-start = ((), (), s32[]{:S(2)}) async-start(), calls=%async_computation.31 | async-start | bytes 2162688 | tf_op jit(solution)/shard_map/reduce_scatter | solution.py:322
  842.6 410.8 %reduce-scatter.20.cloned.1.call-start = ((), (), s32[]{:S(2)}) async-start(), calls=%async_computation.32 | async-start | bytes 4325376 | tf_op jit(solution)/shard_map/reduce_scatter | solution.py:323
  846.2 20.1 copy-start.3
  846.3 552.0 %reduce-scatter.14.cloned.1.call-start = ((), (), s32[]{:S(2)}) async-start(), calls=%async_computation.29 | async-start | bytes 4325376 | tf_op jit(solution)/shard_map/reduce_scatter | solution.py:320
  855.8 16.8 copy-start.5
  868.9 13.0 copy-start.17
  872.4 736.6 %reduce-scatter.22.cloned.1.call-start = ((), (), s32[]{:S(2)}) async-start(), calls=%async_computation.33 | async-start | bytes 19464192 | tf_op jit(solution)/shard_map/reduce_scatter | solution.py:325
  881.9 939.8 %reduce-scatter.24.cloned.1.call-start = ((), (), s32[]{:S(2)}) async-start(), calls=%async_computation.34 | async-start | bytes 19464192 | tf_op jit(solution)/shard_map/reduce_scatter | solution.py:326
  891.2 1143.5 %reduce-scatter.26.cloned.1.call-start = ((), (), s32[]{:S(2)}) async-start(), calls=%async_computation.35 | async-start | bytes 19464192 | tf_op jit(solution)/shard_map/reduce_scatter | solution.py:327
  900.1 48.9 %copy-start.10 = (f32[128,1024]{1,0:T(8,128)S(1)}, f32[128,1024]{1,0:T(8,128)}, u32[]{:S(2)}) copy-start(f32[128,1024]{1,0:T(8,128)} %copy-done.9) | copy-start | bytes 1572868
  (24 other events, 106.6 us)
Sparse Core Ops, SparseCore 0:
  11.0 56.5 all-gather.10
  70.5 52.7 all-gather.12
  126.3 55.3 all-gather.16
  184.3 39.1 all-gather.26
  225.4 38.9 all-gather.28
  267.0 47.7 all-gather.14
  317.8 54.9 all-gather.18
  375.8 80.3 all-gather.20
  459.2 80.0 all-gather.22
  542.1 80.0 all-gather.24
  700.3 62.6 reduce-scatter.9
  766.3 63.1 reduce-scatter.11
  832.2 138.1 reduce-scatter.15
  973.1 135.8 reduce-scatter.17
  1111.7 141.6 reduce-scatter.19
  1256.1 142.1 reduce-scatter.13
  1405.1 203.8 reduce-scatter.21
  1615.8 205.8 reduce-scatter.23
  1828.7 205.9 reduce-scatter.25
